TPU v7x, 32 devices: a whole 2x2x4 slice. The times are simulated.
32 devices in a mesh: kpt: 2 (over x), row: 8 (over z, y), col: 2 (over core).
Axes of the slice: x: 2, y: 2, z: 4, core: 2. Of those that a mesh axis runs over, the one named last changes fastest.
Arguments:
- wannier: float32 [64, 32, 1024], P('kpt', ('row', 'col')), parts along dimension 0, may hold values from -6 to 6
- pairs: int32 [384, 2], replicated, may hold values from 0 to 31, as said below
- gmap: int32 [8192], replicated, may hold values from 1 to 32767, as said below
- screened: bfloat16 [4, 2, 8192, 8192], P('kpt', None, 'row', 'col'), parts along dimension 0, may hold values from -0.046875 to 0.046875
Outputs:
- coulomb: float32 [2, 2, 768, 384], P(None, None, ('kpt', 'row', 'col')), parts along dimension 2
There are 2 independent parts, one for each index of `kpt`. A program takes and returns all parts, laid end to end along the dimension named above; an argument that names none is the same for every part. Nothing has to cross between parts.
Inputs may be any that keep to these rules, and one draw needn't show every extreme that they name: `gmap`: 8192 distinct flat cells of the grid; cell 0 is never among them. `pairs`: in each row the first Wannier function is no greater than the second; no two rows are equal.
All inputs are finite; a program needn't handle non-finite values.
Results may differ from a plain program's by a relative error of at most 0.0082.
Values may be sent and summed in bfloat16 or wider, within the bound.
No kernel may reach another device: no remote copies, remote signals or barrier semaphores. Data moves between devices by JAX's collectives and lax.ppermute only.
A program may use at most 128 MiB of HBM per device.

v0:
```python
import math
import jax
import jax.numpy as jnp
from jax import lax
from jax.sharding import PartitionSpec as P

NW = 32
GX = 32
NG = 8192
NP = 384


def line_tables(side_len):
    positions = jnp.arange(side_len, dtype=jnp.int32)
    phase_index = positions[:, None] * positions[None, :] % side_len
    angles = phase_index.astype(jnp.float32) * (2.0 * math.pi / side_len)
    return (jnp.cos(angles), jnp.sin(angles))


def plane_transform(density):
    cosine, sine_table = line_tables(GX)
    highest = lax.Precision.HIGHEST
    shaped = density.reshape(-1, GX, GX)
    real_z = jnp.einsum("nyz,kz->nyk", shaped, cosine, precision=highest)
    imag_z = -jnp.einsum("nyz,kz->nyk", shaped, sine_table, precision=highest)
    new_real = jnp.einsum("jy,nyk->njk", cosine, real_z, precision=highest) + jnp.einsum(
        "jy,nyk->njk", sine_table, imag_z, precision=highest
    )
    new_imag = jnp.einsum("jy,nyk->njk", cosine, imag_z, precision=highest) - jnp.einsum(
        "jy,nyk->njk", sine_table, real_z, precision=highest
    )
    return (new_real.reshape(density.shape), new_imag.reshape(density.shape))


def line_transform(real_part, imag_part):
    cosine, sine_table = line_tables(GX)
    highest = lax.Precision.HIGHEST
    new_real = jnp.einsum("kn,pny->pky", cosine, real_part, precision=highest) + jnp.einsum(
        "kn,pny->pky", sine_table, imag_part, precision=highest
    )
    new_imag = jnp.einsum("kn,pny->pky", cosine, imag_part, precision=highest) - jnp.einsum(
        "kn,pny->pky", sine_table, real_part, precision=highest
    )
    return (new_real, new_imag)


def right_columns(screened, segment):
    w_real = screened[:, 0]
    w_imag = screened[:, 1]
    real_real = jnp.einsum("fgh,bh->fgb", w_real, segment[0], preferred_element_type=jnp.float32)
    imag_imag = jnp.einsum("fgh,bh->fgb", w_imag, segment[1], preferred_element_type=jnp.float32)
    real_imag = jnp.einsum("fgh,bh->fgb", w_real, segment[1], preferred_element_type=jnp.float32)
    imag_real = jnp.einsum("fgh,bh->fgb", w_imag, segment[0], preferred_element_type=jnp.float32)
    return jnp.stack([real_real - imag_imag, real_imag + imag_real], axis=1)


def shards(wannier, pairs, gmap, screened):
    planes = wannier.shape[1]
    grid_cells = wannier.shape[2]
    members = jnp.arange(NW, dtype=jnp.int32)[None, :]
    pick_first = (pairs[:, 0:1] == members).astype(jnp.float32)
    pick_second = (pairs[:, 1:2] == members).astype(jnp.float32)
    flat_rows = wannier.reshape(NW, -1)
    highest = lax.Precision.HIGHEST
    density = jnp.dot(pick_first, flat_rows, precision=highest) * jnp.dot(
        pick_second, flat_rows, precision=highest
    )
    density = density.reshape(NP, planes, grid_cells)
    arrived = lax.all_to_all(density, ("row", "col"), split_axis=0, concat_axis=1, tiled=True)
    real_part, imag_part = plane_transform(arrived)
    real_part, imag_part = line_transform(real_part, imag_part)
    owned = real_part.shape[0]
    norm_factor = 1.0 / math.sqrt(GX * GX * GX)
    rho_real = jnp.take(real_part.reshape(owned, -1), gmap, axis=1) * norm_factor
    rho_imag = jnp.take(imag_part.reshape(owned, -1), gmap, axis=1) * norm_factor
    rho = jnp.stack([rho_real, rho_imag], axis=0).astype(jnp.bfloat16)
    row_span = screened.shape[2]
    halves = lax.all_to_all(rho, "col", split_axis=2, concat_axis=1, tiled=True)
    screened_rho = right_columns(screened, lax.all_gather(halves, "row", axis=1, tiled=True))
    blocks = lax.all_to_all(rho, "row", split_axis=2, concat_axis=1, tiled=True)
    blocks = blocks.reshape(2, lax.axis_size("row"), owned, row_span)
    left_panel = lax.all_gather(blocks, "col", axis=2, tiled=True).reshape(2, NP, row_span)
    left_wide = left_panel.astype(jnp.float32)
    u_real = jnp.einsum(
        "ag,fgb->fab", left_wide[0], screened_rho[:, 0], precision=highest
    ) + jnp.einsum("ag,fgb->fab", left_wide[1], screened_rho[:, 1], precision=highest)
    u_imag = jnp.einsum(
        "ag,fgb->fab", left_wide[0], screened_rho[:, 1], precision=highest
    ) - jnp.einsum("ag,fgb->fab", left_wide[1], screened_rho[:, 0], precision=highest)
    partial_terms = jnp.stack([u_real, u_imag], axis=1) / math.sqrt(NG)
    summed = lax.psum(partial_terms, ("row", "col"))
    share_rows = NP // lax.axis_size(("row", "col"))
    return lax.dynamic_slice_in_dim(
        summed, lax.axis_index(("row", "col")) * share_rows, share_rows, 2
    )


def solution(mesh):
    return jax.shard_map(
        shards,
        mesh=mesh,
        in_specs=(P("kpt", ("row", "col"), None), P(), P(), P("kpt", None, "row", "col")),
        out_specs=P(None, None, ("kpt", "row", "col"), None),
        check_vma=False,
    )
```

profile of v0, /device:TPU:0, one launch (start us, length us, event | category | flops | bytes accessed | tf_op | source)
XLA Modules:
  0.0 687.3 jit_solution(8600309741713015094)
XLA Ops:
  6.5 0.8 slice_reduce_fusion
  7.3 1.0 copy.93
  8.3 1.4 fusion.54
  9.8 1.5 convolution_multiply_fusion
  11.3 3.8 reshape.35
  15.1 7.5 %all-to-all-start = ((f32[384,2,1024]{2,1,0:T(2,128)}), f32[384,2,1024]{2,1,0:T(2,128)S(1)}, u32[]{:S(2)}, u32[]{:S(2)}) async-start(f32[384,2,1024]{2,1,0:T(2,128)} %reshape.35), calls=%async_computation | async-start | bytes 6291456 | tf_op jit(solution)/shard_map/all_to_all | solution.py:69
  22.6 0.0 all-gather.5.cloned.1.call-start
  22.7 0.0 copy-done.4
  22.7 59.1 %all-to-all-done = f32[384,2,1024]{2,1,0:T(2,128)S(1)} async-done(((f32[384,2,1024]{2,1,0:T(2,128)}), f32[384,2,1024]{2,1,0:T(2,128)S(1)}, u32[]{:S(2)}, u32[]{:S(2)}) %all-to-all-start) | async-done | bytes 3145760 | tf_op jit(solution)/shard_map/all_to_all | solution.py:69
  81.9 1.0 copy.70
  82.9 2.4 copy.71
  85.3 7.6 %reshape.36 = f32[768,32,32]{2,1,0:T(8,128)} reshape(f32[24,16,2,1024]{3,2,1,0:T(2,128)S(1)} %copy.71) | data formatting | bytes 6291456 | tf_op jit(solution)/shard_map/reshape | solution.py:23
  92.9 9.2 %copy.72 = f32[768,32,32]{0,2,1:T(8,128)S(1)} copy(f32[768,32,32]{2,1,0:T(8,128)} %reshape.36) | data formatting | bytes 6291456 | tf_op jit(solution)/shard_map/reshape | solution.py:23
  102.1 3.0 convolution_negate_fusion
  105.1 3.0 fusion.72
  108.1 4.9 fusion.22
  113.1 5.2 fusion.24
  118.2 6.7 add_bitcast_fusion.1
  125.0 5.5 subtract_bitcast_fusion.1
  130.5 10.6 %copy.79 = f32[768,32,32]{2,1,0:T(8,128)} copy(f32[768,32,32]{0,1,2:T(8,128)S(1)} %subtract_bitcast_fusion.1) | data formatting | bytes 6291456 | tf_op jit(solution)/shard_map/sub | solution.py:29
  141.1 9.4 %reshape.38 = f32[24,32,1024]{2,1,0:T(8,128)S(1)} reshape(f32[768,32,32]{2,1,0:T(8,128)} %copy.79) | data formatting | bytes 6291456 | tf_op jit(solution)/shard_map/reshape | solution.py:32
  150.4 5.5 fusion.66
  155.9 11.4 %copy.76 = f32[768,32,32]{2,1,0:T(8,128)} copy(f32[768,32,32]{0,1,2:T(8,128)} %add_bitcast_fusion.1) | data formatting | bytes 6291456 | tf_op jit(solution)/shard_map/add | solution.py:26
  167.3 10.7 %reshape.37 = f32[24,32,1024]{2,1,0:T(8,128)} reshape(f32[768,32,32]{2,1,0:T(8,128)} %copy.76) | data formatting | bytes 6291456 | tf_op jit(solution)/shard_map/reshape | solution.py:32
  178.0 5.9 fusion.69
  184.0 5.5 subtract_bitcast_fusion
  189.5 5.6 add_bitcast_fusion
  195.1 10.3 %copy.89 = f32[24,32,1024]{0,2,1:T(8,128)} copy(f32[24,32,1024]{2,1,0:T(8,128)} %add_bitcast_fusion) | data formatting | bytes 6291456 | tf_op jit(solution)/shard_map/reshape | solution.py:74
  205.4 0.0 copy-done.2
  205.4 8.6 %copy.90 = f32[24,32,1024]{0,2,1:T(8,128)} copy(f32[24,32,1024]{2,1,0:T(8,128)S(1)} %copy-done.2) | data formatting | bytes 6291456 | tf_op jit(solution)/shard_map/reshape | solution.py:75
  214.0 33.6 %gather_fusion = f32[8192,24]{1,0:T(8,128)} fusion(f32[24,32768]{0,1:T(8,128)} %bitcast.144, s32[8192]{0:T(1024)S(1)} %fusion.57), kind=kCustom, calls=%fused_computation.clone | custom fusion | bytes 1605632 | tf_op jit(solution)/shard_map/jit(_take)/gather | solution.py:74
  247.6 33.6 %gather_fusion.1 = f32[8192,24]{1,0:T(8,128)} fusion(f32[24,32768]{0,1:T(8,128)} %bitcast.143, s32[8192]{0:T(1024)S(1)} %fusion.57), kind=kCustom, calls=%fused_computation.1.clone | custom fusion | bytes 1605632 | tf_op jit(solution)/shard_map/jit(_take)/gather | solution.py:75
  281.3 7.2 %fusion.30 = (bf16[1,24,8192]{1,2,0:T(8,128)(2,1)S(1)}, bf16[1,24,8192]{1,2,0:T(8,128)(2,1)S(1)}) fusion(f32[8192,24]{1,0:T(8,128)} %gather_fusion, pred[8192]{0:T(1024)(128)(4,1)S(1)} %compare_and_fusion, f32[8192,24]{1,0:T(8,128)} %gather_fusion.1), kind=kLoop, calls=%fused_computation.43 | loop fusion | flops 1179648 | bytes 2367488 | tf_op jit(solution)/shard_map/stack | solution.py:76
  288.4 0.9 pad_maximum_fusion
  289.4 35.5 %copy.108 = bf16[2,24,8192]{1,0,2:T(2,128)(2,1)} copy(bf16[2,24,8192]{1,2,0:T(8,128)(2,1)S(1)} %pad_maximum_fusion) | data formatting | bytes 1572864 | tf_op jit(solution)/shard_map/stack | solution.py:76
  324.9 6.6 reshape.71
  331.5 35.8 %all_to_all.48 = bf16[8,2,24576]{2,1,0:T(2,128)(2,1)S(1)} all-to-all(bf16[8,2,24576]{2,1,0:T(2,128)(2,1)S(1)} %reshape.71), channel_id=1, replica_groups=mesh['kpt'=2,'row'=8,'col'=2] {'row'}, dimensions={0} | all-to-all | bytes 1572864 | tf_op jit(solution)/shard_map/all_to_all | solution.py:80
  367.3 6.9 %reshape.72 = bf16[8192,2,24]{2,1,0:T(2,128)(2,1)} reshape(bf16[8,2,24576]{2,1,0:T(2,128)(2,1)S(1)} %all_to_all.48) | data formatting | bytes 1572864
  374.3 10.3 %copy.87 = bf16[2,24,8,1024]{3,1,2,0:T(8,128)(2,1)} copy(bf16[2,24,8,1024]{1,0,3,2:T(2,128)(2,1)} %bitcast.145) | data formatting | bytes 1572864 | tf_op jit(solution)/shard_map/all_to_all | solution.py:80
  384.6 0.0 all-gather.5.cloned.1.call-update
  384.6 0.0 all-gather.3.cloned.1.call-start
  384.6 10.2 %copy.109 = bf16[2,24,8192]{1,0,2:T(2,128)(2,1)} copy(bf16[2,24,8192]{1,2,0:T(8,128)(2,1)} %copy-done) | data formatting | bytes 1572864 | tf_op jit(solution)/shard_map/stack | solution.py:76
  394.8 7.0 %reshape.73 = bf16[2,2,98304]{2,1,0:T(2,128)(2,1)S(1)} reshape(bf16[8192,2,24]{2,1,0:T(2,128)(2,1)} %bitcast.147) | data formatting | bytes 1572864
  401.9 4.4 all_to_all.49
  406.2 7.3 %reshape.74 = bf16[8192,2,24]{2,1,0:T(2,128)(2,1)} reshape(bf16[2,2,98304]{2,1,0:T(2,128)(2,1)S(1)} %all_to_all.49) | data formatting | bytes 1572864
  413.6 9.5 %copy.83 = bf16[2,24,2,4096]{3,1,2,0:T(8,128)(2,1)} copy(bf16[2,24,2,4096]{1,0,3,2:T(2,128)(2,1)} %bitcast.146) | data formatting | bytes 1572864 | tf_op jit(solution)/shard_map/all_to_all | solution.py:78
  423.0 0.0 all-gather.3.cloned.1.call-update
  423.1 0.0 all-reduce.2.cloned.1.call-start
  423.1 0.0 all-gather.5.cloned.1.call-done
  423.1 1.5 fusion.129
  424.7 96.3 %all-gather.3.cloned.1.call-done = bf16[2,384,4096]{2,1,0:T(8,128)(2,1)} async-done(((bf16[2,48,4096]{2,1,0:T(8,128)(2,1)}), bf16[2,384,4096]{2,1,0:T(8,128)(2,1)}) %all-gather.3.cloned.1.call-update) | async-done | bytes 6291472 | tf_op jit(solution)/shard_map/all_gather | solution.py:79
  521.0 11.4 %fusion = f32[384,2,1024]{2,0,1:T(8,128)S(1)} fusion(bf16[2,2,1024,4096]{3,2,1,0:T(8,128)(2,1)} %param.9, bf16[2,384,4096]{2,1,0:T(8,128)(2,1)} %all-gather.3.cloned.1.call-done), kind=kOutput, calls=%fused_computation.2 | convolution fusion | flops 6442450944 | bytes 23068672 | tf_op jit(solution)/shard_map/fgh,bh->fgb/dot_general | solution.py:53
  532.4 11.2 %fusion.39 = f32[384,2,1024]{2,0,1:T(8,128)S(1)} fusion(f32[384,2,1024]{2,0,1:T(8,128)S(1)} %fusion, bf16[2,2,1024,4096]{3,2,1,0:T(8,128)(2,1)} %param.9, bf16[2,384,4096]{2,1,0:T(8,128)(2,1)} %all-gather.3.cloned.1.call-done), kind=kOutput, calls=%fused_computation.47 | convolution fusion | flops 6443237376 | bytes 26214400 | tf_op jit(solution)/shard_map/fgh,bh->fgb/dot_general | solution.py:52
  543.6 2.6 fusion.14
  546.2 2.6 fusion.16
  548.9 12.6 %fusion.2 = f32[384,2,1024]{2,0,1:T(8,128)} fusion(bf16[2,2,1024,4096]{3,2,1,0:T(8,128)(2,1)} %param.9, bf16[2,384,4096]{2,1,0:T(8,128)(2,1)} %all-gather.3.cloned.1.call-done), kind=kOutput, calls=%fused_computation.4 | convolution fusion | flops 6442450944 | bytes 23068672 | tf_op jit(solution)/shard_map/fgh,bh->fgb/dot_general | solution.py:51
  561.5 12.1 %fusion.36 = f32[384,2,1024]{2,0,1:T(8,128)S(1)} fusion(f32[384,2,1024]{2,0,1:T(8,128)} %fusion.2, bf16[2,2,1024,4096]{3,2,1,0:T(8,128)(2,1)} %param.9, bf16[2,384,4096]{2,1,0:T(8,128)(2,1)} %all-gather.3.cloned.1.call-done), kind=kOutput, calls=%fused_computation.46 | convolution fusion | flops 6443237376 | bytes 26214400 | tf_op jit(solution)/shard_map/fgh,bh->fgb/dot_general | solution.py:50
  573.6 2.7 fusion.48
  576.3 2.7 fusion.51
  579.0 1.6 maximum_multiply_fusion
  580.6 0.0 all-reduce.2.cloned.1.call-update
  580.6 97.4 %all-reduce.2.cloned.1.call-done = f32[2,2,384,384]{2,3,0,1:T(8,128)} async-done(((f32[2,2,384,384]{2,3,0,1:T(8,128)}), f32[2,2,384,384]{2,3,0,1:T(8,128)}) %all-reduce.2.cloned.1.call-update) | async-done | bytes 2359312 | tf_op jit(solution)/shard_map/psum | solution.py:91
  678.0 1.7 constant_dynamic-slice_fusion
  679.6 0.9 copy.88
  (10 shorter events, 0.0 us)
Async XLA Ops:
  15.1 7.6 %copy-start.4 = (s32[8192]{0:T(1024)S(1)}, s32[8192]{0:T(1024)}, u32[]{:S(2)}) copy-start(s32[8192]{0:T(1024)} %param.8) | copy-start | bytes 98308
  15.1 66.8 %all-to-all-start = ((f32[384,2,1024]{2,1,0:T(2,128)}), f32[384,2,1024]{2,1,0:T(2,128)S(1)}, u32[]{:S(2)}, u32[]{:S(2)}) async-start(f32[384,2,1024]{2,1,0:T(2,128)} %reshape.35), calls=%async_computation | async-start | bytes 6291456 | tf_op jit(solution)/shard_map/all_to_all | solution.py:69
  22.6 400.5 %all-gather.5.cloned.1.call-start = ((), (), s32[]{:S(2)}) async-start(), calls=%async_computation.4 | async-start | bytes 2359296 | tf_op jit(solution)/shard_map/all_gather | solution.py:82
  178.0 6.0 copy-start.1
  178.0 6.0 copy-start.3
  195.1 10.3 %copy-start.2 = (f32[24,32,1024]{2,1,0:T(8,128)S(1)}, f32[24,32,1024]{2,1,0:T(8,128)}, u32[]{:S(2)}) copy-start(f32[24,32,1024]{2,1,0:T(8,128)} %subtract_bitcast_fusion) | copy-start | bytes 9437188
  289.4 35.5 %copy-start = (bf16[2,24,8192]{1,2,0:T(8,128)(2,1)}, bf16[2,24,8192]{1,2,0:T(8,128)(2,1)S(1)}, u32[]{:S(2)}) copy-start(bf16[2,24,8192]{1,2,0:T(8,128)(2,1)S(1)} %pad_maximum_fusion) | copy-start | bytes 2359300
  384.6 136.4 %all-gather.3.cloned.1.call-start = ((), (), s32[]{:S(2)}) async-start(), calls=%async_computation.3 | async-start | bytes 7077888 | tf_op jit(solution)/shard_map/all_gather | solution.py:79
  423.1 254.9 %all-reduce.2.cloned.1.call-start = ((), (), s32[]{:S(2)}) async-start(), calls=%async_computation.5 | async-start | bytes 4718592 | tf_op jit(solution)/shard_map/psum | solution.py:91
Sparse Core Ops, SparseCore 0:
  384.7 8.8 all-gather.4
  423.2 97.7 all-gather.2
  580.7 97.1 all-reduce.1
where the time goes:
time: 696 us; the launch traced here: 687 us
  waiting for transfers between devices  253 us (36%)
  local copies, waits for them, and re-layouts  251 us (36%)
  matrix products  112 us (16%)
  blocking collectives  40.2 us (6%)
  between operations  13.7 us (2%)
  other arithmetic  9.75 us (1%)
  starting transfers between devices  7.67 us (1%)
    psum x1, waiting for transfers between devices, shards(): summed = lax.psum(partial_terms, ('row', 'col'))  97.4 us
    all_gather x1, waiting for transfers between devices, shards(): lax.all_gather(halves, 'row', axis=1, tiled=True)  96.3 us
    all_to_all x1, waiting for transfers between devices, shards(): lax.all_to_all(density, ('row', 'col'), split_axis=0, concat_axis=1, tile...  59.1 us
    another operation x2, local copies, waits for them, and re-layouts, shards(): rho = jnp.stack([rho_real, rho_imag], axis=0).astype(jnp.bfloat16)  45.7 us
    all_to_all x1, blocking collectives, shards(): blocks = lax.all_to_all(rho, 'row', split_axis=2, concat_axis=1, tiled=True)  35.8 us
    gather x1, local copies, waits for them, and re-layouts, shards(): jnp.take(imag_part.reshape(owned, -1), gmap, axis=1) * norm_factor  33.6 us
    gather x1, local copies, waits for them, and re-layouts, shards(): jnp.take(real_part.reshape(owned, -1), gmap, axis=1) * norm_factor  33.6 us
    unnamed x15, local copies, waits for them, and re-layouts  29 us
  transfers between devices with their start and end apart: 4, of which 3 were waited for; matrix products, arithmetic and copies ran while one was open for 5% of the time, Pallas kernels for 0%

commit v1 on v0

--- a/solution.py
+++ b/solution.py
@@ -88,7 +88,7 @@
         "ag,fgb->fab", left_wide[0], screened_rho[:, 1], precision=highest
     ) - jnp.einsum("ag,fgb->fab", left_wide[1], screened_rho[:, 0], precision=highest)
     partial_terms = jnp.stack([u_real, u_imag], axis=1) / math.sqrt(NG)
-    summed = lax.psum(partial_terms, ("row", "col"))
+    summed = jax.lax.psum(jax.lax.psum(partial_terms, "col"), "row")
     share_rows = NP // lax.axis_size(("row", "col"))
     return lax.dynamic_slice_in_dim(
         summed, lax.axis_index(("row", "col")) * share_rows, share_rows, 2

time: 696 us -> 732 us (1.052)
  waiting for transfers between devices: 253 us -> 289 us
    psum x1 -> x2, waiting for transfers between devices: 97.4 us -> 133 us  [shards(): summed = jax.lax.psum(jax.lax.psum(partial_terms, 'col'), 'row')]
  transfers between devices with their start and end apart: 4 -> 5, of which waited for: 3 -> 4; matrix products, arithmetic and copies ran while one was open for 5% -> 5% of each run, Pallas kernels for 0% -> 0%
where the time goes in v1:
time: 732 us; the launch traced here: 723 us
  waiting for transfers between devices  289 us (39%)
  local copies, waits for them, and re-layouts  251 us (34%)
  matrix products  112 us (15%)
  blocking collectives  40.2 us (5%)
  between operations  13.6 us (2%)
  other arithmetic  9.75 us (1%)
  starting transfers between devices  7.71 us (1%)
    psum x2, waiting for transfers between devices, shards(): summed = jax.lax.psum(jax.lax.psum(partial_terms, 'col'), 'row')  133 us
    all_gather x1, waiting for transfers between devices, shards(): lax.all_gather(halves, 'row', axis=1, tiled=True)  96.3 us
    all_to_all x1, waiting for transfers between devices, shards(): lax.all_to_all(density, ('row', 'col'), split_axis=0, concat_axis=1, tile...  59.1 us
    another operation x2, local copies, waits for them, and re-layouts, shards(): rho = jnp.stack([rho_real, rho_imag], axis=0).astype(jnp.bfloat16)  45.7 us
    all_to_all x1, blocking collectives, shards(): blocks = lax.all_to_all(rho, 'row', split_axis=2, concat_axis=1, tiled=True)  35.8 us
    gather x1, local copies, waits for them, and re-layouts, shards(): jnp.take(imag_part.reshape(owned, -1), gmap, axis=1) * norm_factor  33.6 us
    gather x1, local copies, waits for them, and re-layouts, shards(): jnp.take(real_part.reshape(owned, -1), gmap, axis=1) * norm_factor  33.6 us
    unnamed x15, local copies, waits for them, and re-layouts  29 us
  transfers between devices with their start and end apart: 5, of which 4 were waited for; matrix products, arithmetic and copies ran while one was open for 5% of the time, Pallas kernels for 0%

profile of v1, /device:TPU:0, one launch (start us, length us, event | category | flops | bytes accessed | tf_op | source)
XLA Modules:
  0.0 723.0 jit_solution(16120302236635844372)
XLA Ops:
  6.5 0.8 slice_reduce_fusion
  7.3 1.0 copy.93
  8.3 1.4 fusion.54
  9.8 1.5 convolution_multiply_fusion
  11.3 3.8 reshape.35
  15.1 7.5 %all-to-all-start = ((f32[384,2,1024]{2,1,0:T(2,128)}), f32[384,2,1024]{2,1,0:T(2,128)S(1)}, u32[]{:S(2)}, u32[]{:S(2)}) async-start(f32[384,2,1024]{2,1,0:T(2,128)} %reshape.35), calls=%async_computation | async-start | bytes 6291456 | tf_op jit(solution)/shard_map/all_to_all | solution.py:69
  22.6 0.0 all-gather.5.cloned.1.call-start
  22.7 59.1 %all-to-all-done = f32[384,2,1024]{2,1,0:T(2,128)S(1)} async-done(((f32[384,2,1024]{2,1,0:T(2,128)}), f32[384,2,1024]{2,1,0:T(2,128)S(1)}, u32[]{:S(2)}, u32[]{:S(2)}) %all-to-all-start) | async-done | bytes 3145760 | tf_op jit(solution)/shard_map/all_to_all | solution.py:69
  81.9 1.0 copy.70
  82.9 2.4 copy.71
  85.3 7.6 %reshape.36 = f32[768,32,32]{2,1,0:T(8,128)} reshape(f32[24,16,2,1024]{3,2,1,0:T(2,128)S(1)} %copy.71) | data formatting | bytes 6291456 | tf_op jit(solution)/shard_map/reshape | solution.py:23
  92.9 9.2 %copy.72 = f32[768,32,32]{0,2,1:T(8,128)S(1)} copy(f32[768,32,32]{2,1,0:T(8,128)} %reshape.36) | data formatting | bytes 6291456 | tf_op jit(solution)/shard_map/reshape | solution.py:23
  102.1 3.0 convolution_negate_fusion
  105.1 3.0 fusion.72
  108.1 4.9 fusion.22
  113.1 5.2 fusion.24
  118.2 6.7 add_bitcast_fusion.1
  125.0 5.5 subtract_bitcast_fusion.1
  130.5 10.6 %copy.79 = f32[768,32,32]{2,1,0:T(8,128)} copy(f32[768,32,32]{0,1,2:T(8,128)S(1)} %subtract_bitcast_fusion.1) | data formatting | bytes 6291456 | tf_op jit(solution)/shard_map/sub | solution.py:29
  141.1 9.4 %reshape.38 = f32[24,32,1024]{2,1,0:T(8,128)S(1)} reshape(f32[768,32,32]{2,1,0:T(8,128)} %copy.79) | data formatting | bytes 6291456 | tf_op jit(solution)/shard_map/reshape | solution.py:32
  150.4 5.5 fusion.66
  155.9 11.4 %copy.76 = f32[768,32,32]{2,1,0:T(8,128)} copy(f32[768,32,32]{0,1,2:T(8,128)} %add_bitcast_fusion.1) | data formatting | bytes 6291456 | tf_op jit(solution)/shard_map/add | solution.py:26
  167.3 10.7 %reshape.37 = f32[24,32,1024]{2,1,0:T(8,128)} reshape(f32[768,32,32]{2,1,0:T(8,128)} %copy.76) | data formatting | bytes 6291456 | tf_op jit(solution)/shard_map/reshape | solution.py:32
  178.0 5.9 fusion.69
  184.0 5.5 subtract_bitcast_fusion
  189.5 5.6 add_bitcast_fusion
  195.1 10.3 %copy.89 = f32[24,32,1024]{0,2,1:T(8,128)} copy(f32[24,32,1024]{2,1,0:T(8,128)} %add_bitcast_fusion) | data formatting | bytes 6291456 | tf_op jit(solution)/shard_map/reshape | solution.py:74
  205.4 8.6 %copy.90 = f32[24,32,1024]{0,2,1:T(8,128)} copy(f32[24,32,1024]{2,1,0:T(8,128)S(1)} %copy-done.2) | data formatting | bytes 6291456 | tf_op jit(solution)/shard_map/reshape | solution.py:75
  214.0 33.6 %gather_fusion = f32[8192,24]{1,0:T(8,128)} fusion(f32[24,32768]{0,1:T(8,128)} %bitcast.144, s32[8192]{0:T(1024)S(1)} %fusion.57), kind=kCustom, calls=%fused_computation.clone | custom fusion | bytes 1605632 | tf_op jit(solution)/shard_map/jit(_take)/gather | solution.py:74
  247.6 33.6 %gather_fusion.1 = f32[8192,24]{1,0:T(8,128)} fusion(f32[24,32768]{0,1:T(8,128)} %bitcast.143, s32[8192]{0:T(1024)S(1)} %fusion.57), kind=kCustom, calls=%fused_computation.1.clone | custom fusion | bytes 1605632 | tf_op jit(solution)/shard_map/jit(_take)/gather | solution.py:75
  281.3 7.2 fusion.30
  288.4 0.9 pad_maximum_fusion
  289.4 35.5 %copy.108 = bf16[2,24,8192]{1,0,2:T(2,128)(2,1)} copy(bf16[2,24,8192]{1,2,0:T(8,128)(2,1)S(1)} %pad_maximum_fusion) | data formatting | bytes 1572864 | tf_op jit(solution)/shard_map/stack | solution.py:76
  324.9 6.6 reshape.71
  331.5 35.8 %all_to_all.48 = bf16[8,2,24576]{2,1,0:T(2,128)(2,1)S(1)} all-to-all(bf16[8,2,24576]{2,1,0:T(2,128)(2,1)S(1)} %reshape.71), channel_id=1, replica_groups=mesh['kpt'=2,'row'=8,'col'=2] {'row'}, dimensions={0} | all-to-all | bytes 1572864 | tf_op jit(solution)/shard_map/all_to_all | solution.py:80
  367.3 6.9 reshape.72
  374.3 10.3 %copy.87 = bf16[2,24,8,1024]{3,1,2,0:T(8,128)(2,1)} copy(bf16[2,24,8,1024]{1,0,3,2:T(2,128)(2,1)} %bitcast.145) | data formatting | bytes 1572864 | tf_op jit(solution)/shard_map/all_to_all | solution.py:80
  384.6 0.0 all-gather.5.cloned.1.call-update
  384.6 0.0 all-gather.3.cloned.1.call-start
  384.6 10.2 %copy.109 = bf16[2,24,8192]{1,0,2:T(2,128)(2,1)} copy(bf16[2,24,8192]{1,2,0:T(8,128)(2,1)} %copy-done) | data formatting | bytes 1572864 | tf_op jit(solution)/shard_map/stack | solution.py:76
  394.8 7.0 reshape.73
  401.9 4.4 all_to_all.49
  406.2 7.3 %reshape.74 = bf16[8192,2,24]{2,1,0:T(2,128)(2,1)} reshape(bf16[2,2,98304]{2,1,0:T(2,128)(2,1)S(1)} %all_to_all.49) | data formatting | bytes 1572864
  413.6 9.5 %copy.83 = bf16[2,24,2,4096]{3,1,2,0:T(8,128)(2,1)} copy(bf16[2,24,2,4096]{1,0,3,2:T(2,128)(2,1)} %bitcast.146) | data formatting | bytes 1572864 | tf_op jit(solution)/shard_map/all_to_all | solution.py:78
  423.0 0.0 all-gather.3.cloned.1.call-update
  423.1 0.0 all-reduce.3.cloned.1.call-start
  423.1 0.0 all-gather.5.cloned.1.call-done
  423.1 1.5 fusion.129
  424.7 96.3 %all-gather.3.cloned.1.call-done = bf16[2,384,4096]{2,1,0:T(8,128)(2,1)} async-done(((bf16[2,48,4096]{2,1,0:T(8,128)(2,1)}), bf16[2,384,4096]{2,1,0:T(8,128)(2,1)}) %all-gather.3.cloned.1.call-update) | async-done | bytes 6291472 | tf_op jit(solution)/shard_map/all_gather | solution.py:79
  521.0 11.4 %fusion = f32[384,2,1024]{2,0,1:T(8,128)S(1)} fusion(bf16[2,2,1024,4096]{3,2,1,0:T(8,128)(2,1)} %param.9, bf16[2,384,4096]{2,1,0:T(8,128)(2,1)} %all-gather.3.cloned.1.call-done), kind=kOutput, calls=%fused_computation.2 | convolution fusion | flops 6442450944 | bytes 23068672 | tf_op jit(solution)/shard_map/fgh,bh->fgb/dot_general | solution.py:53
  532.3 11.2 %fusion.39 = f32[384,2,1024]{2,0,1:T(8,128)S(1)} fusion(f32[384,2,1024]{2,0,1:T(8,128)S(1)} %fusion, bf16[2,2,1024,4096]{3,2,1,0:T(8,128)(2,1)} %param.9, bf16[2,384,4096]{2,1,0:T(8,128)(2,1)} %all-gather.3.cloned.1.call-done), kind=kOutput, calls=%fused_computation.47 | convolution fusion | flops 6443237376 | bytes 26214400 | tf_op jit(solution)/shard_map/fgh,bh->fgb/dot_general | solution.py:52
  543.6 2.6 fusion.14
  546.2 2.6 fusion.16
  548.9 12.6 %fusion.2 = f32[384,2,1024]{2,0,1:T(8,128)} fusion(bf16[2,2,1024,4096]{3,2,1,0:T(8,128)(2,1)} %param.9, bf16[2,384,4096]{2,1,0:T(8,128)(2,1)} %all-gather.3.cloned.1.call-done), kind=kOutput, calls=%fused_computation.4 | convolution fusion | flops 6442450944 | bytes 23068672 | tf_op jit(solution)/shard_map/fgh,bh->fgb/dot_general | solution.py:51
  561.5 11.9 %fusion.36 = f32[384,2,1024]{2,0,1:T(8,128)S(1)} fusion(f32[384,2,1024]{2,0,1:T(8,128)} %fusion.2, bf16[2,2,1024,4096]{3,2,1,0:T(8,128)(2,1)} %param.9, bf16[2,384,4096]{2,1,0:T(8,128)(2,1)} %all-gather.3.cloned.1.call-done), kind=kOutput, calls=%fused_computation.46 | convolution fusion | flops 6443237376 | bytes 26214400 | tf_op jit(solution)/shard_map/fgh,bh->fgb/dot_general | solution.py:50
  573.3 2.7 fusion.48
  576.0 2.7 fusion.51
  578.7 1.6 maximum_multiply_fusion
  580.3 0.0 all-reduce.5.cloned.1.call-start
  580.4 20.0 %all-reduce.3.cloned.1.call-done = f32[2,2,384,384]{2,3,0,1:T(8,128)} async-done(((f32[2,2,384,384]{2,3,0,1:T(8,128)}), f32[2,2,384,384]{2,3,0,1:T(8,128)}) %all-reduce.3.cloned.1.call-update) | async-done | bytes 2359312 | tf_op jit(solution)/shard_map/psum | solution.py:91
  600.4 0.0 all-reduce.5.cloned.1.call-update
  600.4 113.2 %all-reduce.5.cloned.1.call-done = f32[2,2,384,384]{2,3,0,1:T(8,128)} async-done(((f32[2,2,384,384]{2,3,0,1:T(8,128)}), f32[2,2,384,384]{2,3,0,1:T(8,128)}) %all-reduce.5.cloned.1.call-update) | async-done | bytes 2359312 | tf_op jit(solution)/shard_map/psum | solution.py:91
  713.6 1.7 constant_dynamic-slice_fusion
  715.3 0.9 copy.88
  (13 shorter events, 0.1 us)
Async XLA Ops:
  15.1 7.6 %copy-start.4 = (s32[8192]{0:T(1024)S(1)}, s32[8192]{0:T(1024)}, u32[]{:S(2)}) copy-start(s32[8192]{0:T(1024)} %param.8) | copy-start | bytes 98308
  15.1 66.8 %all-to-all-start = ((f32[384,2,1024]{2,1,0:T(2,128)}), f32[384,2,1024]{2,1,0:T(2,128)S(1)}, u32[]{:S(2)}, u32[]{:S(2)}) async-start(f32[384,2,1024]{2,1,0:T(2,128)} %reshape.35), calls=%async_computation | async-start | bytes 6291456 | tf_op jit(solution)/shard_map/all_to_all | solution.py:69
  22.6 400.5 %all-gather.5.cloned.1.call-start = ((), (), s32[]{:S(2)}) async-start(), calls=%async_computation.4 | async-start | bytes 2359296 | tf_op jit(solution)/shard_map/all_gather | solution.py:82
  178.0 6.0 copy-start.1
  178.0 6.0 copy-start.3
  195.1 10.3 %copy-start.2 = (f32[24,32,1024]{2,1,0:T(8,128)S(1)}, f32[24,32,1024]{2,1,0:T(8,128)}, u32[]{:S(2)}) copy-start(f32[24,32,1024]{2,1,0:T(8,128)} %subtract_bitcast_fusion) | copy-start | bytes 9437188
  289.4 35.5 %copy-start = (bf16[2,24,8192]{1,2,0:T(8,128)(2,1)}, bf16[2,24,8192]{1,2,0:T(8,128)(2,1)S(1)}, u32[]{:S(2)}) copy-start(bf16[2,24,8192]{1,2,0:T(8,128)(2,1)S(1)} %pad_maximum_fusion) | copy-start | bytes 2359300
  384.6 136.4 %all-gather.3.cloned.1.call-start = ((), (), s32[]{:S(2)}) async-start(), calls=%async_computation.3 | async-start | bytes 7077888 | tf_op jit(solution)/shard_map/all_gather | solution.py:79
  423.1 177.3 %all-reduce.3.cloned.1.call-start = ((), (), s32[]{:S(2)}) async-start(), calls=%async_computation.5 | async-start | bytes 4718592 | tf_op jit(solution)/shard_map/psum | solution.py:91
  580.3 133.3 %all-reduce.5.cloned.1.call-start = ((), (), s32[]{:S(2)}) async-start(), calls=%async_computation.6 | async-start | bytes 4718592 | tf_op jit(solution)/shard_map/psum | solution.py:91
Sparse Core Ops, SparseCore 0:
  384.7 8.8 all-gather.4
  423.2 97.7 all-gather.2
  580.5 19.9 all-reduce.2
  603.8 109.7 all-reduce.4
